TPU v7x, 32 devices: a whole 2x2x4 slice. The times are simulated.
32 devices in a mesh: rep: 2 (over x), tp: 4 (over y, core), sub: 4 (over z).
Axes of the slice: x: 2, y: 2, z: 4, core: 2. Of those that a mesh axis runs over, the one named last changes fastest.
Arguments:
- acts: bfloat16 [2048, 16384], P(('rep', 'tp'), 'sub'), parts along dimension 0, may hold values from -6 to 6
- q_src: bfloat16 [32768, 16384], P(('rep', 'sub'), 'tp'), parts along dimension 0, may hold values from -0.046875 to 0.046875
- kv_src: bfloat16 [32768, 2048], P(('rep', 'sub'), 'tp'), parts along dimension 0, may hold values from -0.046875 to 0.046875
- q_src_heads: int32 [128], replicated, may hold values from 0 to 127, as said below
- q_tgt_heads: int32 [128], replicated, may hold values from 0 to 127, as said below
- kv_tgt_heads: int32 [16], replicated, may hold values from 0 to 7, as said below
Outputs:
- q_new: bfloat16 [32768, 16384], P(('rep', 'sub'), 'tp'), parts along dimension 0
- kv_new: bfloat16 [32768, 4096], P(('rep', 'sub'), 'tp'), parts along dimension 0
- qkv: bfloat16 [2048, 20480], P(('rep', 'sub'), 'tp'), parts along dimension 0
There are 2 independent parts, one for each index of `rep`. A program takes and returns all parts, laid end to end along the dimension named above; an argument that names none is the same for every part. Nothing has to cross between parts.
Inputs may be any that keep to these rules, and one draw needn't show every extreme that they name: q_src_heads and q_tgt_heads are permutations. Source block t is entries t * 32 to (t + 1) * 32 - 1 of q_src_heads, target block j the same entries of q_tgt_heads. With s = 1, source block t shares exactly 8 heads with target block (t + min(1, s - 1)) mod 4 and with each target block (t + k * s) mod 4 for k from 1 to 3, and none with any other. `q_tgt_heads`: see q_src_heads. `kv_tgt_heads`: every key-value head appears exactly twice.
All inputs are finite; a program needn't handle non-finite values.
Results may differ from a plain program's by a relative error of at most 0.001.
Values may be sent and summed in bfloat16 or wider, within the bound.
A program may use at most 256 MiB of HBM per device.

v0:
```python
import jax
import jax.numpy as jnp
from jax import lax
from jax.sharding import PartitionSpec as P

HD = 128


def per_device(acts, q_src, kv_src, q_src_heads, q_tgt_heads, kv_tgt_heads):
    tp_count = lax.axis_size("tp")
    my_index = lax.axis_index("tp")
    row_count = q_src.shape[0]
    q_local = q_src.shape[1] // HD
    capacity = max(2, q_local // tp_count)
    head_count = q_src_heads.shape[0]
    head_ids = jnp.arange(head_count, dtype=jnp.int32)
    matches = (q_src_heads[None, :] == q_tgt_heads[:, None]).astype(jnp.int32)
    target_pos = jnp.sum(matches * head_ids[:, None], axis=0)
    slot_of = jnp.sum(matches * head_ids[None, :], axis=1)
    target_dev = target_pos // q_local
    source_dev = head_ids // q_local
    earlier = (
        (source_dev[:, None] == source_dev[None, :])
        & (target_dev[:, None] == target_dev[None, :])
        & (head_ids[None, :] < head_ids[:, None])
    )
    slot_rank = jnp.sum(earlier.astype(jnp.int32), axis=1)
    own_target = lax.dynamic_slice_in_dim(target_dev, my_index * q_local, q_local)
    own_rank = lax.dynamic_slice_in_dim(slot_rank, my_index * q_local, q_local)
    buffer_ids = jnp.arange(tp_count * capacity, dtype=jnp.int32)
    slot_hit = ((own_target * capacity + own_rank)[None, :] == buffer_ids[:, None]).astype(
        jnp.int32
    )
    pick_slot = jnp.sum(slot_hit * jnp.arange(q_local, dtype=jnp.int32)[None, :], axis=1)
    filled = jnp.sum(slot_hit, axis=1) > 0
    my_slots = lax.dynamic_slice_in_dim(slot_of, my_index * q_local, q_local)
    receive_ids = my_slots // q_local * capacity + slot_rank[my_slots]

    def pack_heads(weights):
        leading = weights.shape[0]
        three = weights.reshape(leading, q_local, HD)
        packed = jnp.take(three, pick_slot, axis=1) * filled[None, :, None].astype(weights.dtype)
        return packed.reshape(leading, tp_count, capacity * HD)

    def unpack_heads(arrived):
        leading = arrived.shape[0]
        three = arrived.reshape(leading, tp_count * capacity, HD)
        return jnp.take(three, receive_ids, axis=1).reshape(leading, q_local * HD)

    q_arrived = lax.all_to_all(pack_heads(q_src), "tp", split_axis=1, concat_axis=1, tiled=True)
    q_new = unpack_heads(q_arrived)
    kv_slots = kv_tgt_heads.shape[0] // tp_count
    kv_whole = lax.all_gather(kv_src, "tp", axis=1, tiled=True)
    own_kv = lax.dynamic_slice_in_dim(kv_tgt_heads, my_index * kv_slots, kv_slots)
    kv_three = kv_whole.reshape(row_count, kv_whole.shape[1] // (2 * HD), 2 * HD)
    kv_new = jnp.take(kv_three, own_kv, axis=1).reshape(row_count, kv_slots * 2 * HD)
    gathered = lax.all_gather(acts, "tp", axis=0, tiled=True)

    def projector(weights):
        return jnp.dot(gathered, weights, preferred_element_type=jnp.float32)

    q_out = lax.psum_scatter(projector(q_src), "sub", scatter_dimension=0, tiled=True).astype(
        jnp.bfloat16
    )
    q_moved = lax.all_to_all(pack_heads(q_out), "tp", split_axis=1, concat_axis=1, tiled=True)
    kv_out = lax.psum_scatter(projector(kv_new), "sub", scatter_dimension=0, tiled=True).astype(
        jnp.bfloat16
    )
    qkv = jnp.concatenate([unpack_heads(q_moved), kv_out], axis=1)
    return (q_new, kv_new, qkv)


def solution(mesh):
    in_specs = (
        P(("rep", "tp"), "sub"),
        P(("rep", "sub"), "tp"),
        P(("rep", "sub"), "tp"),
        P(),
        P(),
        P(),
    )
    out_specs = (P(("rep", "sub"), "tp"), P(("rep", "sub"), "tp"), P(("rep", "sub"), "tp"))
    return jax.shard_map(
        per_device, mesh=mesh, in_specs=in_specs, out_specs=out_specs, check_vma=False
    )
```

profile of v0, /device:TPU:0, one launch (start us, length us, event | category | flops | bytes accessed | tf_op | source)
XLA Modules:
  0.0 703.1 jit_solution(10137896972993409188)
XLA Ops:
  7.2 0.0 all-gather.5.cloned.1.call-start
  7.2 0.7 all-gather.5.cloned.1.call-update
  7.9 0.0 all-gather.3.cloned.1.call-start
  7.9 0.7 all-gather.3.cloned.1.call-update
  8.6 0.0 reduce-scatter.3.cloned.1.call-start
  8.7 61.9 %all-gather.5.cloned.1.call-done = bf16[1024,4096]{1,0:T(8,128)(2,1)} async-done(((bf16[256,4096]{1,0:T(8,128)(2,1)}), bf16[1024,4096]{1,0:T(8,128)(2,1)}) %all-gather.5.cloned.1.call-update) | async-done | bytes 8388624 | tf_op jit(solution)/shard_map/all_gather | solution.py:57
  70.6 43.0 %fusion.4 = f32[1024,4096]{1,0:T(8,128)} fusion(bf16[1024,4096]{1,0:T(8,128)(2,1)} %all-gather.5.cloned.1.call-done, bf16[4096,4096]{1,0:T(8,128)(2,1)} %param.11), kind=kOutput, calls=%fused_computation.53 | convolution fusion | flops 34359738368 | bytes 58720256 | tf_op jit(solution)/shard_map/dot_general | solution.py:60
  113.5 0.0 reduce-scatter.3.cloned.1.call-update
  113.6 0.0 copy-start
  113.6 0.0 copy-start.1
  113.6 44.2 %copy.27 = bf16[4096,4096]{0,1:T(8,128)(2,1)} copy(bf16[4096,4096]{1,0:T(8,128)(2,1)} %param.11) | data formatting | bytes 67108864 | tf_op args[1]
  157.7 0.0 copy-done
  157.7 0.0 copy-done.1
  157.8 0.2 fusion.1
  157.9 0.2 convert_reduce_fusion
  158.1 0.1 dynamic-slice_add_fusion
  158.2 0.1 convert_reduce_fusion.1
  158.4 22.9 %gather_fusion.3 = bf16[32,4096,128]{1,2,0:T(8,128)(2,1)} fusion(bf16[4096,32,128]{0,2,1:T(8,128)(2,1)} %bitcast.31, s32[1024]{0:T(1024)S(1)} %pad_clamp_fusion.2), kind=kCustom, calls=%fused_computation.clone | custom fusion | bytes 67108992 | tf_op jit(solution)/shard_map/jit(_take)/gather | solution.py:42
  181.3 22.3 %bitcast_multiply_fusion = bf16[4096,32,128]{0,2,1:T(8,128)(2,1)} fusion(bf16[32,4096,128]{1,2,0:T(8,128)(2,1)} %gather_fusion.3, pred[32]{0:T(512)(128)(4,1)S(1)} %compare_and_fusion.1, bf16[32]{0:T(256)(128)(2,1)S(1)} %compare_convert_fusion), kind=kLoop, calls=%fused_computation.7 | loop fusion | flops 33554432 | bytes 67108960 | tf_op jit(solution)/shard_map/mul | solution.py:42
  203.5 0.0 copy-start.2
  203.5 9.9 %all-to-all-start = ((bf16[4096,4,1024]{0,2,1:T(8,128)(2,1)}), bf16[4096,4,1024]{0,2,1:T(8,128)(2,1)}, u32[]{:S(2)}, u32[]{:S(2)}) async-start(bf16[4096,4,1024]{0,2,1:T(8,128)(2,1)} %bitcast.33), calls=%async_computation | async-start | bytes 67108864 | tf_op jit(solution)/shard_map/all_to_all | solution.py:50
  213.5 0.2 reduce-scatter.5.cloned.1.call-start
  213.7 0.0 copy-done.2
  213.7 0.1 compare_and_fusion.2
  213.8 0.1 broadcast_in_dim.53
  213.9 0.0 all-gather.3.cloned.1.call-done
  213.9 12.0 %fusion.3 = (bf16[2048,2048]{1,0:T(8,128)(2,1)}, bf16[2048,2048]{1,0:T(8,128)(2,1)}) fusion(bf16[4096,2048]{1,0:T(8,128)(2,1)} %all-gather.3.cloned.1.call-done), kind=kLoop, calls=%fused_computation.52 | loop fusion | bytes 33554432 | tf_op jit(solution)/shard_map/jit(_take)/gather | solution.py:56
  226.0 12.3 %copy.29 = bf16[2048,2048]{0,1:T(8,128)(2,1)} copy(bf16[2048,2048]{1,0:T(8,128)(2,1)} %get-tuple-element.23) | data formatting | bytes 16777216 | tf_op jit(solution)/shard_map/jit(_take)/gather | solution.py:56
  238.2 12.5 %copy.28 = bf16[2048,2048]{0,1:T(8,128)(2,1)} copy(bf16[2048,2048]{1,0:T(8,128)(2,1)} %get-tuple-element.22) | data formatting | bytes 16777216 | tf_op jit(solution)/shard_map/jit(_take)/gather | solution.py:56
  250.7 6.5 gather_fusion.2
  257.1 6.4 gather_fusion.1
  263.5 8.0 %pad_maximum_fusion = bf16[4096,4,256]{0,2,1:T(8,128)(2,1)} fusion(bf16[2048,4,256]{0,2,1:T(8,128)(2,1)} %bitcast.37, bf16[2048,4,256]{0,2,1:T(8,128)(2,1)} %bitcast.38), kind=kLoop, calls=%fused_computation.9 | loop fusion | flops 16777216 | bytes 16777216
  271.5 12.0 %copy.30 = bf16[4096,1024]{1,0:T(8,128)(2,1)} copy(bf16[4096,1024]{0,1:T(8,128)(2,1)} %bitcast.34) | data formatting | bytes 16777216 | tf_op jit(solution)/shard_map/jit(_take)/gather | solution.py:56
  283.4 7.5 %broadcast_select_fusion.1 = bf16[4096,1024]{1,0:T(8,128)(2,1)} fusion(bf16[4096,1024]{1,0:T(8,128)(2,1)} %copy.30, pred[1024]{0:T(1024)(128)(4,1)S(1)} %broadcast_in_dim.54), kind=kLoop, calls=%fused_computation.10 | loop fusion | flops 4194304 | bytes 16778240 | tf_op jit(solution)/shard_map/jit(_take)/select_n | solution.py:56
  290.9 15.2 %convolution_bitcast_fusion = f32[1024,1024]{0,1:T(8,128)} fusion(bf16[4096,1024]{1,0:T(8,128)(2,1)} %broadcast_select_fusion.1, bf16[1024,4096]{1,0:T(8,128)(2,1)} %all-gather.5.cloned.1.call-done), kind=kOutput, calls=%fused_computation.12 | convolution fusion | flops 8589934592 | bytes 20971520 | tf_op jit(solution)/shard_map/dot_general | solution.py:60
  306.2 0.0 reduce-scatter.5.cloned.1.call-update
  306.2 0.1 compare_select_fusion.5
  306.3 0.7 gather_fusion
  307.0 0.1 compare_and_fusion
  307.1 269.2 %all-to-all-done = bf16[4096,4,1024]{0,2,1:T(8,128)(2,1)} async-done(((bf16[4096,4,1024]{0,2,1:T(8,128)(2,1)}), bf16[4096,4,1024]{0,2,1:T(8,128)(2,1)}, u32[]{:S(2)}, u32[]{:S(2)}) %all-to-all-start) | async-done | bytes 33554464 | tf_op jit(solution)/shard_map/all_to_all | solution.py:50
  576.3 23.0 %gather_fusion.4 = bf16[32,4096,128]{1,2,0:T(8,128)(2,1)} fusion(bf16[4096,32,128]{0,2,1:T(8,128)(2,1)} %bitcast.3, s32[1024]{0:T(1024)S(1)} %pad_clamp_fusion.1), kind=kCustom, calls=%fused_computation.2.clone | custom fusion | bytes 67108992 | tf_op jit(solution)/shard_map/jit(_take)/gather | solution.py:48
  599.3 0.0 reduce-scatter.3.cloned.1.call-done
  599.3 2.7 copy_bitcast_fusion
  602.0 2.1 gather_fusion.5
  604.1 1.9 bitcast_multiply_fusion.1
  606.0 2.9 copy.32
  608.9 3.8 all-to-all-start.1
  612.8 22.8 %broadcast_select_fusion = bf16[32,4096,128]{1,2,0:T(8,128)(2,1)} fusion(bf16[32,4096,128]{1,2,0:T(8,128)(2,1)} %gather_fusion.4, pred[32]{0:T(512)(128)(4,1)S(1)} %get-tuple-element.20), kind=kLoop, calls=%fused_computation.8 | loop fusion | flops 16777216 | bytes 67108896 | tf_op jit(solution)/shard_map/jit(_take)/select_n | solution.py:48
  635.6 44.1 %copy.35 = bf16[4096,4096]{1,0:T(8,128)(2,1)} copy(bf16[4096,4096]{0,1:T(8,128)(2,1)} %bitcast.32) | data formatting | bytes 67108864
  679.7 0.0 reduce-scatter.5.cloned.1.call-done
  679.7 1.3 convert_element_type.26
  681.0 0.0 all-to-all-done.1
  681.0 2.9 copy.33
  683.8 2.5 gather_fusion.6
  686.4 1.6 select_bitcast_fusion
  688.0 4.1 copy.34
  692.0 1.8 pad_maximum_fusion.1
  693.8 2.8 copy.36
  (9 shorter events, 0.1 us)
Async XLA Ops:
  7.2 63.4 %all-gather.5.cloned.1.call-start = ((), (), s32[]{:S(2)}) async-start(), calls=%async_computation.5 | async-start | bytes 10485760 | tf_op jit(solution)/shard_map/all_gather | solution.py:57
  7.9 206.0 %all-gather.3.cloned.1.call-start = ((), (), s32[]{:S(2)}) async-start(), calls=%async_computation.4 | async-start | bytes 20971520 | tf_op jit(solution)/shard_map/all_gather | solution.py:53
  8.6 590.7 %reduce-scatter.3.cloned.1.call-start = ((), (), s32[]{:S(2)}) async-start(), calls=%async_computation.6 | async-start | bytes 20971520 | tf_op jit(solution)/shard_map/reduce_scatter | solution.py:62
  113.6 44.2 %copy-start = (s32[128]{0:T(128)S(1)}, s32[128]{0:T(128)}, u32[]{:S(2)}) copy-start(s32[128]{0:T(128)} %param.13) | copy-start | bytes 1540
  113.6 44.2 %copy-start.1 = (s32[128]{0:T(128)S(1)}, s32[128]{0:T(128)}, u32[]{:S(2)}) copy-start(s32[128]{0:T(128)} %param.14) | copy-start | bytes 1540
  203.5 10.2 %copy-start.2 = (s32[16]{0:T(128)S(1)}, s32[16]{0:T(128)}, u32[]{:S(2)}) copy-start(s32[16]{0:T(128)} %param.15) | copy-start | bytes 196
  203.5 372.7 %all-to-all-start = ((bf16[4096,4,1024]{0,2,1:T(8,128)(2,1)}), bf16[4096,4,1024]{0,2,1:T(8,128)(2,1)}, u32[]{:S(2)}, u32[]{:S(2)}) async-start(bf16[4096,4,1024]{0,2,1:T(8,128)(2,1)} %bitcast.33), calls=%async_computation | async-start | bytes 67108864 | tf_op jit(solution)/shard_map/all_to_all | solution.py:50
  213.5 466.2 %reduce-scatter.5.cloned.1.call-start = ((), (), s32[]{:S(2)}) async-start(), calls=%async_computation.7 | async-start | bytes 5242880 | tf_op jit(solution)/shard_map/reduce_scatter | solution.py:66
  608.9 72.0 %all-to-all-start.1 = ((bf16[256,4,1024]{0,2,1:T(8,128)(2,1)}), bf16[256,4,1024]{0,2,1:T(8,128)(2,1)S(1)}, u32[]{:S(2)}, u32[]{:S(2)}) async-start(bf16[256,4,1024]{0,2,1:T(8,128)(2,1)} %bitcast.40), calls=%async_computation.2 | async-start | bytes 4194304 | tf_op jit(solution)/shard_map/all_to_all | solution.py:65
Sparse Core Ops, SparseCore 0:
  9.5 60.9 all-gather.4
  72.1 105.8 all-gather.2
  180.4 280.4 reduce-scatter.2
  463.0 77.3 reduce-scatter.4
where the time goes:
time: 707 us; the launch traced here: 703 us
  waiting for transfers between devices  332 us (47%)
  local copies, waits for them, and re-layouts  214 us (30%)
  other arithmetic  70.6 us (10%)
  matrix products  58.2 us (8%)
  starting transfers between devices  14.1 us (2%)
  between operations  13.9 us (2%)
    all_to_all x1, waiting for transfers between devices, per_device(): lax.all_to_all(pack_heads(q_src), 'tp', split_axis=1, concat_axis=1, tile...  269 us
    unnamed x9, local copies, waits for them, and re-layouts  91 us
    all_gather x1, waiting for transfers between devices, per_device(): gathered = lax.all_gather(acts, 'tp', axis=0, tiled=True)  61.9 us
    gather x6, local copies, waits for them, and re-layouts, per_device(): jnp.take(kv_three, own_kv, axis=1).reshape(row_count, kv_slots * 2 * HD)  61.5 us
    dot_general x2, matrix products, projector(): return jnp.dot(gathered, weights, preferred_element_type=jnp.float32)  58.2 us
    gather x2, local copies, waits for them, and re-layouts, unpack_heads(): return jnp.take(three, receive_ids, axis=1).reshape(leading, q_local * HD)  25.6 us
    gather x2, local copies, waits for them, and re-layouts, pack_heads(): jnp.take(three, pick_slot, axis=1)  25 us
    select_n x2, other arithmetic, unpack_heads(): return jnp.take(three, receive_ids, axis=1).reshape(leading, q_local * HD)  24.4 us
  transfers between devices with their start and end apart: 6, of which 2 were waited for; matrix products, arithmetic and copies ran while one was open for 47% of the time, Pallas kernels for 0%

commit v1 on v0

--- a/solution.py
+++ b/solution.py
@@ -47,7 +47,12 @@
         three = arrived.reshape(leading, tp_count * capacity, HD)
         return jnp.take(three, receive_ids, axis=1).reshape(leading, q_local * HD)
 
-    q_arrived = lax.all_to_all(pack_heads(q_src), "tp", split_axis=1, concat_axis=1, tiled=True)
+    q_arrived = jnp.concatenate(
+        lax.all_to_all(
+            jnp.stack(jnp.split(pack_heads(q_src), lax.axis_size("tp"), axis=1)), "tp", 0, 0
+        ),
+        axis=1,
+    )
     q_new = unpack_heads(q_arrived)
     kv_slots = kv_tgt_heads.shape[0] // tp_count
     kv_whole = lax.all_gather(kv_src, "tp", axis=1, tiled=True)

time: 707 us -> 844 us (1.19)
  local copies, waits for them, and re-layouts: 214 us -> 326 us
  other arithmetic: 70.6 us -> 95.5 us
    unnamed x9 -> x25, local copies, waits for them, and re-layouts: 91 us -> 140 us
    reshape x0 -> x1, local copies, waits for them, and re-layouts: none -> 40.5 us  [per_device(): jnp.concatenate(lax.all_to_all(jnp.stack(jnp.split(pack_heads(q_src), lax...]
    split x0 -> x1, local copies, waits for them, and re-layouts: none -> 23.2 us  [per_device(): jnp.split(pack_heads(q_src), lax.axis_size('tp'), axis=1)]
    another operation x0 -> x1, other arithmetic: none -> 22.8 us  [per_device(): jnp.stack(jnp.split(pack_heads(q_src), lax.axis_size('tp'), axis=1))]
  transfers between devices with their start and end apart: 6 -> 6, of which waited for: 2 -> 2; matrix products, arithmetic and copies ran while one was open for 47% -> 55% of each run, Pallas kernels for 0% -> 0%
where the time goes in v1:
time: 844 us; the launch traced here: 838 us
  waiting for transfers between devices  330 us (39%)
  local copies, waits for them, and re-layouts  326 us (39%)
  other arithmetic  95.5 us (11%)
  matrix products  58.4 us (7%)
  between operations  14 us (2%)
  starting transfers between devices  13.9 us (2%)
    all_to_all x1, waiting for transfers between devices, per_device(): lax.all_to_all(jnp.stack(jnp.split(pack_heads(q_src), lax.axis_size('tp')...  269 us
    unnamed x25, local copies, waits for them, and re-layouts  140 us
    gather x6, local copies, waits for them, and re-layouts, per_device(): jnp.take(kv_three, own_kv, axis=1).reshape(row_count, kv_slots * 2 * HD)  61.3 us
    all_gather x1, waiting for transfers between devices, per_device(): gathered = lax.all_gather(acts, 'tp', axis=0, tiled=True)  59.7 us
    dot_general x2, matrix products, projector(): return jnp.dot(gathered, weights, preferred_element_type=jnp.float32)  58.4 us
    reshape x1, local copies, waits for them, and re-layouts, per_device(): jnp.concatenate(lax.all_to_all(jnp.stack(jnp.split(pack_heads(q_src), lax...  40.5 us
    gather x2, local copies, waits for them, and re-layouts, unpack_heads(): return jnp.take(three, receive_ids, axis=1).reshape(leading, q_local * HD)  25.4 us
    gather x2, local copies, waits for them, and re-layouts, pack_heads(): jnp.take(three, pick_slot, axis=1)  25.1 us
  transfers between devices with their start and end apart: 6, of which 2 were waited for; matrix products, arithmetic and copies ran while one was open for 55% of the time, Pallas kernels for 0%

profile of v1, /device:TPU:0, one launch (start us, length us, event | category | flops | bytes accessed | tf_op | source)
XLA Modules:
  0.0 837.9 jit_solution(7530825441867822553)
XLA Ops:
  7.2 0.0 all-gather.5.cloned.1.call-start
  7.2 0.7 all-gather.5.cloned.1.call-update
  7.9 0.0 all-gather.3.cloned.1.call-start
  7.9 0.7 all-gather.3.cloned.1.call-update
  8.6 0.0 reduce-scatter.3.cloned.1.call-start
  8.7 1.4 fusion.1
  10.1 0.2 convert_reduce_fusion
  10.3 0.5 copy-done
  10.7 0.1 dynamic-slice_add_fusion
  10.8 59.7 %all-gather.5.cloned.1.call-done = bf16[1024,4096]{1,0:T(8,128)(2,1)} async-done(((bf16[256,4096]{1,0:T(8,128)(2,1)}), bf16[1024,4096]{1,0:T(8,128)(2,1)}) %all-gather.5.cloned.1.call-update) | async-done | bytes 8388624 | tf_op jit(solution)/shard_map/all_gather | solution.py:62
  70.6 43.0 %fusion.5 = f32[1024,4096]{1,0:T(8,128)} fusion(bf16[1024,4096]{1,0:T(8,128)(2,1)} %all-gather.5.cloned.1.call-done, bf16[4096,4096]{1,0:T(8,128)(2,1)} %param.11), kind=kOutput, calls=%fused_computation.55 | convolution fusion | flops 34359738368 | bytes 58720256 | tf_op jit(solution)/shard_map/dot_general | solution.py:65
  113.5 0.0 reduce-scatter.3.cloned.1.call-update
  113.5 0.1 convert_reduce_fusion.1
  113.7 44.1 %copy.40 = bf16[4096,4096]{0,1:T(8,128)(2,1)} copy(bf16[4096,4096]{1,0:T(8,128)(2,1)} %param.11) | data formatting | bytes 67108864 | tf_op args[1]
  157.8 22.9 %gather_fusion.3 = bf16[32,4096,128]{1,2,0:T(8,128)(2,1)} fusion(bf16[4096,32,128]{0,2,1:T(8,128)(2,1)} %bitcast.36, s32[1024]{0:T(1024)S(1)} %pad_clamp_fusion.2), kind=kCustom, calls=%fused_computation.clone | custom fusion | bytes 67108992 | tf_op jit(solution)/shard_map/jit(_take)/gather | solution.py:42
  180.7 0.0 copy-done.2
  180.7 0.0 copy-start.4
  180.7 0.0 copy-start.6
  180.7 23.2 %bitcast_multiply_fusion = bf16[4096,32,128]{0,2,1:T(8,128)(2,1)} fusion(bf16[32,4096,128]{1,2,0:T(8,128)(2,1)} %gather_fusion.3, pred[32]{0:T(512)(128)(4,1)S(1)} %compare_and_fusion.1, bf16[32]{0:T(256)(128)(2,1)S(1)} %compare_convert_fusion), kind=kLoop, calls=%fused_computation.8 | loop fusion | flops 33554432 | bytes 67108960 | tf_op jit(solution)/shard_map/mul | solution.py:42
  203.9 0.0 copy-done.4
  204.0 23.2 %fusion.3 = (bf16[4096,1,1024]{0,2,1:T(8,128)(2,1)}, bf16[4096,1,1024]{0,2,1:T(8,128)(2,1)}, bf16[4096,1,1024]{0,2,1:T(8,128)(2,1)}, bf16[4096,1,1024]{0,2,1:T(8,128)(2,1)}) fusion(bf16[4096,4,1024]{0,2,1:T(8,128)(2,1)} %bitcast.39), kind=kLoop, calls=%fused_computation.53 | loop fusion | bytes 67108864 | tf_op jit(solution)/shard_map/split | solution.py:52
  227.2 12.0 %copy.58 = bf16[4096,1,1024]{2,0,1:T(8,128)(2,1)} copy(bf16[4096,1,1024]{0,2,1:T(8,128)(2,1)} %get-tuple-element.25) | data formatting | bytes 16777216
  239.2 12.0 %copy.57 = bf16[4096,1,1024]{2,0,1:T(8,128)(2,1)} copy(bf16[4096,1,1024]{0,2,1:T(8,128)(2,1)} %get-tuple-element.23) | data formatting | bytes 16777216
  251.2 12.1 %copy.56 = bf16[4096,1,1024]{2,0,1:T(8,128)(2,1)} copy(bf16[4096,1,1024]{0,2,1:T(8,128)(2,1)} %get-tuple-element.24) | data formatting | bytes 16777216
  263.3 11.9 %copy.55 = bf16[4096,1,1024]{2,0,1:T(8,128)(2,1)} copy(bf16[4096,1,1024]{0,2,1:T(8,128)(2,1)} %get-tuple-element.22) | data formatting | bytes 16777216
  275.3 22.8 %pad_maximum_fusion = bf16[4,4096,1,1024]{3,1,2,0:T(8,128)(2,1)} fusion(bf16[1,4096,1,1024]{3,1,2,0:T(8,128)(2,1)} %bitcast.41, bf16[1,4096,1,1024]{3,1,2,0:T(8,128)(2,1)} %bitcast.42, bf16[1,4096,1,1024]{3,1,2,0:T(8,128)(2,1)} %bitcast.43, bf16[1,4096,1,1024]{3,1,2,0:T(8,128)(2,1)} %bitcast.44), kind=kLoop, calls=%fused_computation.7 | loop fusion | flops 50331648 | bytes 67108864 | tf_op jit(solution)/shard_map/stack | solution.py:52
  298.1 0.0 copy-start.8
  298.1 9.8 %all-to-all-start = ((bf16[4,4096,1,1024]{3,1,2,0:T(8,128)(2,1)}), bf16[4,4096,1,1024]{3,1,2,0:T(8,128)(2,1)}, u32[]{:S(2)}, u32[]{:S(2)}) async-start(bf16[4,4096,1,1024]{3,1,2,0:T(8,128)(2,1)} %pad_maximum_fusion), calls=%async_computation | async-start | bytes 67108864 | tf_op jit(solution)/shard_map/all_to_all | solution.py:51
  307.9 0.2 reduce-scatter.5.cloned.1.call-start
  308.1 0.1 compare_and_fusion.2
  308.2 0.1 broadcast_in_dim.53
  308.3 0.0 all-gather.3.cloned.1.call-done
  308.3 12.1 %fusion.4 = (bf16[2048,2048]{1,0:T(8,128)(2,1)}, bf16[2048,2048]{1,0:T(8,128)(2,1)}) fusion(bf16[4096,2048]{1,0:T(8,128)(2,1)} %all-gather.3.cloned.1.call-done), kind=kLoop, calls=%fused_computation.54 | loop fusion | bytes 33554432 | tf_op jit(solution)/shard_map/jit(_take)/gather | solution.py:61
  320.4 12.4 %copy.47 = bf16[2048,2048]{0,1:T(8,128)(2,1)} copy(bf16[2048,2048]{1,0:T(8,128)(2,1)} %get-tuple-element.27) | data formatting | bytes 16777216 | tf_op jit(solution)/shard_map/jit(_take)/gather | solution.py:61
  332.8 12.4 %copy.46 = bf16[2048,2048]{0,1:T(8,128)(2,1)} copy(bf16[2048,2048]{1,0:T(8,128)(2,1)} %get-tuple-element.26) | data formatting | bytes 16777216 | tf_op jit(solution)/shard_map/jit(_take)/gather | solution.py:61
  345.2 6.2 gather_fusion.2
  351.4 6.2 gather_fusion.1
  357.6 8.0 pad_maximum_fusion.1
  365.6 12.1 %copy.48 = bf16[4096,1024]{1,0:T(8,128)(2,1)} copy(bf16[4096,1024]{0,1:T(8,128)(2,1)} %bitcast.40) | data formatting | bytes 16777216 | tf_op jit(solution)/shard_map/jit(_take)/gather | solution.py:61
  377.6 7.5 broadcast_select_fusion.1
  385.1 15.4 %convolution_bitcast_fusion = f32[1024,1024]{0,1:T(8,128)} fusion(bf16[4096,1024]{1,0:T(8,128)(2,1)} %broadcast_select_fusion.1, bf16[1024,4096]{1,0:T(8,128)(2,1)} %all-gather.5.cloned.1.call-done), kind=kOutput, calls=%fused_computation.13 | convolution fusion | flops 8589934592 | bytes 20971520 | tf_op jit(solution)/shard_map/dot_general | solution.py:65
  400.5 0.0 reduce-scatter.5.cloned.1.call-update
  400.6 0.1 compare_select_fusion.5
  400.7 0.7 gather_fusion
  401.4 0.1 compare_and_fusion
  401.5 269.2 %all-to-all-done = bf16[4,4096,1,1024]{3,1,2,0:T(8,128)(2,1)} async-done(((bf16[4,4096,1,1024]{3,1,2,0:T(8,128)(2,1)}), bf16[4,4096,1,1024]{3,1,2,0:T(8,128)(2,1)}, u32[]{:S(2)}, u32[]{:S(2)}) %all-to-all-start) | async-done | bytes 33554464 | tf_op jit(solution)/shard_map/all_to_all | solution.py:51
  670.7 40.5 %copy.45 = bf16[4096,4,1,1024]{0,3,1,2:T(8,128)(2,1)} copy(bf16[4096,4,1,1024]{3,0,2,1:T(8,128)(2,1)} %bitcast.7) | data formatting | bytes 67108864 | tf_op jit(solution)/shard_map/reshape | solution.py:50
  711.1 22.8 %gather_fusion.4 = bf16[32,4096,128]{1,2,0:T(8,128)(2,1)} fusion(bf16[4096,32,128]{0,2,1:T(8,128)(2,1)} %bitcast.37, s32[1024]{0:T(1024)S(1)} %pad_clamp_fusion.1), kind=kCustom, calls=%fused_computation.2.clone | custom fusion | bytes 67108992 | tf_op jit(solution)/shard_map/jit(_take)/gather | solution.py:48
  734.0 2.7 copy_bitcast_fusion
  736.7 2.3 gather_fusion.5
  739.0 0.0 copy-done.5
  739.0 1.9 bitcast_multiply_fusion.1
  740.9 2.9 copy.50
  743.7 3.8 all-to-all-start.1
  747.6 22.8 %broadcast_select_fusion = bf16[32,4096,128]{1,2,0:T(8,128)(2,1)} fusion(bf16[32,4096,128]{1,2,0:T(8,128)(2,1)} %gather_fusion.4, pred[32]{0:T(512)(128)(4,1)S(1)} %get-tuple-element.20), kind=kLoop, calls=%fused_computation.9 | loop fusion | flops 16777216 | bytes 67108896 | tf_op jit(solution)/shard_map/jit(_take)/select_n | solution.py:48
  770.4 44.1 %copy.53 = bf16[4096,4096]{1,0:T(8,128)(2,1)} copy(bf16[4096,4096]{0,1:T(8,128)(2,1)} %bitcast.38) | data formatting | bytes 67108864
  814.5 1.3 convert_element_type.26
  815.8 0.0 all-to-all-done.1
  815.8 2.9 copy.51
  818.7 2.5 gather_fusion.6
  821.2 1.6 select_bitcast_fusion
  822.8 4.1 copy.52
  826.8 1.8 pad_maximum_fusion.2
  828.6 2.8 copy.54
  (22 shorter events, 0.1 us)
Async XLA Ops:
  7.2 63.4 %all-gather.5.cloned.1.call-start = ((), (), s32[]{:S(2)}) async-start(), calls=%async_computation.5 | async-start | bytes 10485760 | tf_op jit(solution)/shard_map/all_gather | solution.py:62
  7.9 300.4 %all-gather.3.cloned.1.call-start = ((), (), s32[]{:S(2)}) async-start(), calls=%async_computation.4 | async-start | bytes 20971520 | tf_op jit(solution)/shard_map/all_gather | solution.py:58
  8.6 725.3 %reduce-scatter.3.cloned.1.call-start = ((), (), s32[]{:S(2)}) async-start(), calls=%async_computation.6 | async-start | bytes 20971520 | tf_op jit(solution)/shard_map/reduce_scatter | solution.py:67
  10.3 0.5 copy-start
  157.8 22.9 %copy-start.2 = (s32[1024]{0:T(1024)}, s32[1024]{0:T(1024)S(1)}, u32[]{:S(2)}) copy-start(s32[1024]{0:T(1024)S(1)} %pad_clamp_fusion.2) | copy-start | bytes 12292
  180.7 23.2 %copy-start.4 = (pred[32]{0:T(512)(128)(4,1)}, pred[32]{0:T(512)(128)(4,1)S(1)}, u32[]{:S(2)}) copy-start(pred[32]{0:T(512)(128)(4,1)S(1)} %compare_and_fusion.1) | copy-start | bytes 100
  180.7 23.2 %copy-start.6 = (bf16[32]{0:T(256)(128)(2,1)}, bf16[32]{0:T(256)(128)(2,1)S(1)}, u32[]{:S(2)}) copy-start(bf16[32]{0:T(256)(128)(2,1)S(1)} %compare_convert_fusion) | copy-start | bytes 196
  298.1 10.0 %copy-start.8 = (s32[16]{0:T(128)S(1)}, s32[16]{0:T(128)}, u32[]{:S(2)}) copy-start(s32[16]{0:T(128)} %param.15) | copy-start | bytes 196
  298.1 372.6 %all-to-all-start = ((bf16[4,4096,1,1024]{3,1,2,0:T(8,128)(2,1)}), bf16[4,4096,1,1024]{3,1,2,0:T(8,128)(2,1)}, u32[]{:S(2)}, u32[]{:S(2)}) async-start(bf16[4,4096,1,1024]{3,1,2,0:T(8,128)(2,1)} %pad_maximum_fusion), calls=%async_computation | async-start | bytes 67108864 | tf_op jit(solution)/shard_map/all_to_all | solution.py:51
  307.9 506.6 %reduce-scatter.5.cloned.1.call-start = ((), (), s32[]{:S(2)}) async-start(), calls=%async_computation.7 | async-start | bytes 5242880 | tf_op jit(solution)/shard_map/reduce_scatter | solution.py:71
  385.1 15.4 %copy-start.3 = (s32[128]{0:T(128)S(1)}, s32[128]{0:T(128)}, u32[]{:S(2)}) copy-start(s32[128]{0:T(128)} %get-tuple-element.14) | copy-start | bytes 1540
  385.1 15.5 %copy-start.1 = (s32[128]{0:T(128)S(1)}, s32[128]{0:T(128)}, u32[]{:S(2)}) copy-start(s32[128]{0:T(128)} %copy-done) | copy-start | bytes 1540
  734.0 5.0 copy-start.5
  734.0 5.0 copy-start.7
  743.7 72.0 %all-to-all-start.1 = ((bf16[256,4,1024]{0,2,1:T(8,128)(2,1)}), bf16[256,4,1024]{0,2,1:T(8,128)(2,1)S(1)}, u32[]{:S(2)}, u32[]{:S(2)}) async-start(bf16[256,4,1024]{0,2,1:T(8,128)(2,1)} %bitcast.50), calls=%async_computation.2 | async-start | bytes 4194304 | tf_op jit(solution)/shard_map/all_to_all | solution.py:70
Sparse Core Ops, SparseCore 0:
  9.5 60.9 all-gather.4
  72.1 105.8 all-gather.2
  180.4 280.4 reduce-scatter.2
  463.0 77.3 reduce-scatter.4
